TPU v7x, 8 devices: a whole 2x2x1 slice. The times are simulated.
8 devices in a mesh: dp: 2 (over z, y), tp: 4 (over x, core).
Axes of the slice: x: 2, y: 2, z: 1, core: 2. Of those that a mesh axis runs over, the one named last changes fastest.
Arguments:
- hidden: bfloat16 [6, 1024, 8192], P('dp', 'tp'), parts along dimension 0
- attn_gain: float32 [8192], replicated
- attn_bias: float32 [8192], replicated
- mlp_gain: float32 [8192], replicated
- mlp_bias: float32 [8192], replicated
- w_qkv: bfloat16 [8192, 8, 1152], P(None, 'tp')
- w_out: bfloat16 [8192, 8192], P('tp')
- w_up: bfloat16 [8192, 32768], P(None, 'tp')
- w_down: bfloat16 [32768, 8192], P('tp')
- positions: int32 [1024], replicated
Outputs:
- output: bfloat16 [6, 1024, 8192], P('dp', 'tp'), parts along dimension 0
There are 2 independent parts. A program takes and returns all parts, laid end to end along the dimension named above; an argument that names none is the same for every part.
All inputs are finite; a program needn't handle non-finite values.
Results may differ from a plain program's by a relative error of at most 0.00657843.
Values are sent between devices in bfloat16 or wider.
A program may use at most 1.5 GiB of HBM per device.

v0:
```python
import jax
import jax.numpy as jnp
from jax import lax
from jax.sharding import PartitionSpec as P


def layer_norm(tok_rows, norm_gain, norm_bias):
    rows32 = tok_rows.astype(jnp.float32)
    row_mean = jnp.mean(rows32, axis=-1, keepdims=True)
    centered = rows32 - row_mean
    row_var = jnp.mean(centered * centered, axis=-1, keepdims=True)
    return (centered * lax.rsqrt(row_var + 1e-5) * norm_gain + norm_bias).astype(jnp.bfloat16)


def rotary_tables(positions, head_dim):
    inv_freq = 10000.0 ** (-2.0 * jnp.arange(head_dim // 2, dtype=jnp.float32) / head_dim)
    angles = positions.astype(jnp.float32)[:, None] * inv_freq[None, :]
    angles = jnp.concatenate([angles, angles], axis=-1)
    return jnp.cos(angles), jnp.sin(angles)


def apply_rotary(head_vals, cos_tab, sin_tab):
    half_dim = head_vals.shape[-1] // 2
    vals32 = head_vals.astype(jnp.float32)
    rotated = jnp.concatenate([-vals32[..., half_dim:], vals32[..., :half_dim]], axis=-1)
    return (vals32 * cos_tab + rotated * sin_tab).astype(jnp.bfloat16)


def attention_branch(normed, w_qkv_part, w_out_part, positions):
    batch_size, seq_len, model_width = normed.shape
    num_groups = w_qkv_part.shape[1]
    slot_cols = w_qkv_part.shape[2]
    group_cols = w_out_part.shape[0] // num_groups
    head_dim = (slot_cols - group_cols) // 2
    group_size = group_cols // head_dim
    qkv_rows = jnp.einsum('bsd,dkc->bskc', normed, w_qkv_part, preferred_element_type=jnp.float32).astype(jnp.bfloat16)
    qkv_rows = qkv_rows.reshape(batch_size, seq_len, num_groups, group_size + 2, head_dim)
    cos_tab, sin_tab = rotary_tables(positions, head_dim)
    query_rot = apply_rotary(qkv_rows[:, :, :, :group_size, :], cos_tab[None, :, None, None, :], sin_tab[None, :, None, None, :])
    key_rot = apply_rotary(qkv_rows[:, :, :, group_size, :], cos_tab[None, :, None, :], sin_tab[None, :, None, :])
    value_seq = qkv_rows[:, :, :, group_size + 1, :]
    block_len = min(seq_len, 256)
    num_blocks = seq_len // block_len
    key_idx = jnp.arange(seq_len)
    score_scale = head_dim ** -0.5

    def one_block(block_idx):
        row_start = block_idx * block_len
        query_blk = lax.dynamic_slice_in_dim(query_rot, row_start, block_len, axis=1)
        scores = jnp.einsum('bqkgh,bskh->bkgqs', query_blk, key_rot, preferred_element_type=jnp.float32) * score_scale
        query_idx = row_start + jnp.arange(block_len)
        allowed = key_idx[None, :] <= query_idx[:, None]
        scores = jnp.where(allowed, scores, -1e30)
        exp_scores = jnp.exp(scores - jnp.max(scores, axis=-1, keepdims=True))
        attn_probs = (exp_scores / jnp.sum(exp_scores, axis=-1, keepdims=True)).astype(jnp.bfloat16)
        context = jnp.einsum('bkgqs,bskh->bqkgh', attn_probs, value_seq, preferred_element_type=jnp.float32)
        return context.astype(jnp.bfloat16).reshape(batch_size, block_len, num_groups * group_cols)

    ctx_blocks = lax.map(one_block, jnp.arange(num_blocks))
    attn_part = jnp.einsum('nbqc,cd->bnqd', ctx_blocks, w_out_part, preferred_element_type=jnp.float32)
    return attn_part.reshape(batch_size, seq_len, model_width)


def solution(mesh):
    def local_layer(hidden_blk, attn_gain, attn_bias, mlp_gain, mlp_bias, w_qkv_part, w_out_part, w_up_part, w_down_part, positions):
        normed_attn = layer_norm(hidden_blk, attn_gain, attn_bias)
        normed_mlp = layer_norm(hidden_blk, mlp_gain, mlp_bias)
        attn_in = lax.all_gather(normed_attn, 'tp', axis=1, tiled=True)
        mlp_in = lax.all_gather(normed_mlp, 'tp', axis=1, tiled=True)
        attn_part = attention_branch(attn_in, w_qkv_part, w_out_part, positions)
        up_pre = jnp.einsum('bsd,df->bsf', mlp_in, w_up_part, preferred_element_type=jnp.float32)
        up_act = jax.nn.gelu(up_pre, approximate=False).astype(jnp.bfloat16)
        mlp_part = jnp.einsum('bsf,fd->bsd', up_act, w_down_part, preferred_element_type=jnp.float32)
        token_sum = lax.psum_scatter(attn_part + mlp_part, 'tp', scatter_dimension=1, tiled=True)
        return (hidden_blk.astype(jnp.float32) + token_sum).astype(jnp.bfloat16)

    return jax.shard_map(local_layer, mesh=mesh, in_specs=(P('dp', 'tp', None), P(), P(), P(), P(), P(None, 'tp', None), P('tp', None), P(None, 'tp'), P('tp', None), P()), out_specs=P('dp', 'tp', None), check_vma=False)
```

profile of v0, /device:TPU:0, one launch (start us, length us, event | category | flops | bytes accessed | tf_op | source)
XLA Modules:
  0.0 2946.3 jit_solution(10883745899115944308)
XLA Ops:
  20.9 15.9 fusion.93
  40.3 294.0 %all-gather.3.cloned.1.call-done = bf16[3,1024,8192]{2,1,0:T(8,128)(2,1)} async-done(((bf16[3,256,8192]{2,1,0:T(8,128)(2,1)}), bf16[3,1024,8192]{2,1,0:T(8,128)(2,1)}) %all-gather.3.cloned.1.call-update) | async-done | bytes 50331664 | tf_op jit(solution)/shard_map/all_gather | solution.py:68
  334.3 132.1 %fusion.100 = bf16[3,1024,2,1152]{3,1,2,0:T(8,128)(2,1)} fusion(bf16[8192,2,1152]{2,1,0:T(2,128)(2,1)} %param.17, bf16[3,1024,8192]{2,1,0:T(8,128)(2,1)} %all-gather.3.cloned.1.call-done), kind=kOutput, calls=%fused_computation.109 | convolution fusion | flops 115971194880 | bytes 102236160 | tf_op jit(solution)/shard_map/bsd,dkc->bskc/dot_general | solution.py:36
  466.4 18.7 copy.18
  487.7 14.6 slice_convert_fusion
  502.5 20.8 slice_negate_fusion
  525.8 15.4 fusion.97
  541.7 323.1 %while.11 = (s32[]{:T(128)}, bf16[4,3,256,2048]{2,3,1,0:T(8,128)(2,1)}, s32[4]{0:T(128)}, bf16[3,1024,2,16,64]{1,4,3,2,0:T(8,128)(2,1)}, bf16[3,1024,2,64]{1,3,2...) while((s32[]{:T(128)}, ...), condition=%wide.region_5.6_spmd.clone, body=%wide.region_2.5_spmd.clone.sunk | while | flops 6595281920 | bytes 216205488 | solution.py:59
  544.0 43.3 %fusion.167 = (f32[3,2,16,256]{3,2,1,0:T(8,128)S(1)}, f32[3,2,16,256,1024]{4,3,2,1,0:T(8,128)}) fusion(pred[256,1024]{1,0:T(8,128)(4,1)S(1)} %iota_compare_fusion.2, bf16[3,1024,2,16,64]{1,4,3,2,0:T(8,128)(2,1)} %get-tuple-element.147, s32[]{:T(128)S(6)} %select_n.28, bf16[3,1024,2,64]{1,3,2,0:T(8,128)(2,1)} %get-tuple-element.148), kind=kOutput, calls=%fused_computation.159.clone.1 | convolution fusion | flops 3321889792 | bytes 104955904 | tf_op jit(solution)/shard_map/while/body/eval_jaxpr/sub | solution.py:54
  587.2 33.3 %fusion.168 = bf16[3,2,16,256,64]{3,4,2,1,0:T(8,128)(2,1)S(1)} fusion(f32[3,2,16,256,1024]{4,3,2,1,0:T(8,128)} %get-tuple-element.122, f32[3,2,16,256]{3,2,1,0:T(8,128)S(1)} %get-tuple-element.123, bf16[3,1024,2,64]{1,3,2,0:T(8,128)(2,1)} %get-tuple-element.149), kind=kOutput, calls=%fused_computation.16.clone.1 | convolution fusion | flops 3273129984 | bytes 104693760 | tf_op jit(solution)/shard_map/while/body/eval_jaxpr/bkgqs,bskh->bqkgh/dot_general | solution.py:56
  624.6 43.3 %fusion.167 = (f32[3,2,16,256]{3,2,1,0:T(8,128)S(1)}, f32[3,2,16,256,1024]{4,3,2,1,0:T(8,128)}) fusion(pred[256,1024]{1,0:T(8,128)(4,1)S(1)} %iota_compare_fusion.2, bf16[3,1024,2,16,64]{1,4,3,2,0:T(8,128)(2,1)} %get-tuple-element.147, s32[]{:T(128)S(6)} %select_n.28, bf16[3,1024,2,64]{1,3,2,0:T(8,128)(2,1)} %get-tuple-element.148), kind=kOutput, calls=%fused_computation.159.clone.1 | convolution fusion | flops 3321889792 | bytes 104955904 | tf_op jit(solution)/shard_map/while/body/eval_jaxpr/sub | solution.py:54
  667.9 33.3 %fusion.168 = bf16[3,2,16,256,64]{3,4,2,1,0:T(8,128)(2,1)S(1)} fusion(f32[3,2,16,256,1024]{4,3,2,1,0:T(8,128)} %get-tuple-element.122, f32[3,2,16,256]{3,2,1,0:T(8,128)S(1)} %get-tuple-element.123, bf16[3,1024,2,64]{1,3,2,0:T(8,128)(2,1)} %get-tuple-element.149), kind=kOutput, calls=%fused_computation.16.clone.1 | convolution fusion | flops 3273129984 | bytes 104693760 | tf_op jit(solution)/shard_map/while/body/eval_jaxpr/bkgqs,bskh->bqkgh/dot_general | solution.py:56
  705.3 43.3 %fusion.167 = (f32[3,2,16,256]{3,2,1,0:T(8,128)S(1)}, f32[3,2,16,256,1024]{4,3,2,1,0:T(8,128)}) fusion(pred[256,1024]{1,0:T(8,128)(4,1)S(1)} %iota_compare_fusion.2, bf16[3,1024,2,16,64]{1,4,3,2,0:T(8,128)(2,1)} %get-tuple-element.147, s32[]{:T(128)S(6)} %select_n.28, bf16[3,1024,2,64]{1,3,2,0:T(8,128)(2,1)} %get-tuple-element.148), kind=kOutput, calls=%fused_computation.159.clone.1 | convolution fusion | flops 3321889792 | bytes 104955904 | tf_op jit(solution)/shard_map/while/body/eval_jaxpr/sub | solution.py:54
  748.6 33.3 %fusion.168 = bf16[3,2,16,256,64]{3,4,2,1,0:T(8,128)(2,1)S(1)} fusion(f32[3,2,16,256,1024]{4,3,2,1,0:T(8,128)} %get-tuple-element.122, f32[3,2,16,256]{3,2,1,0:T(8,128)S(1)} %get-tuple-element.123, bf16[3,1024,2,64]{1,3,2,0:T(8,128)(2,1)} %get-tuple-element.149), kind=kOutput, calls=%fused_computation.16.clone.1 | convolution fusion | flops 3273129984 | bytes 104693760 | tf_op jit(solution)/shard_map/while/body/eval_jaxpr/bkgqs,bskh->bqkgh/dot_general | solution.py:56
  786.0 43.3 %fusion.167 = (f32[3,2,16,256]{3,2,1,0:T(8,128)S(1)}, f32[3,2,16,256,1024]{4,3,2,1,0:T(8,128)}) fusion(pred[256,1024]{1,0:T(8,128)(4,1)S(1)} %iota_compare_fusion.2, bf16[3,1024,2,16,64]{1,4,3,2,0:T(8,128)(2,1)} %get-tuple-element.147, s32[]{:T(128)S(6)} %select_n.28, bf16[3,1024,2,64]{1,3,2,0:T(8,128)(2,1)} %get-tuple-element.148), kind=kOutput, calls=%fused_computation.159.clone.1 | convolution fusion | flops 3321889792 | bytes 104955904 | tf_op jit(solution)/shard_map/while/body/eval_jaxpr/sub | solution.py:54
  829.3 33.3 %fusion.168 = bf16[3,2,16,256,64]{3,4,2,1,0:T(8,128)(2,1)S(1)} fusion(f32[3,2,16,256,1024]{4,3,2,1,0:T(8,128)} %get-tuple-element.122, f32[3,2,16,256]{3,2,1,0:T(8,128)S(1)} %get-tuple-element.123, bf16[3,1024,2,64]{1,3,2,0:T(8,128)(2,1)} %get-tuple-element.149), kind=kOutput, calls=%fused_computation.16.clone.1 | convolution fusion | flops 3273129984 | bytes 104693760 | tf_op jit(solution)/shard_map/while/body/eval_jaxpr/bkgqs,bskh->bqkgh/dot_general | solution.py:56
  864.9 500.1 %fusion.98 = (u8[1024,8192]{1,0:T(8,128)(4,1)}, f32[3,1024,8192]{2,1,0:T(8,128)}) fusion(bf16[3,1024,8192]{2,1,0:T(8,128)(2,1)} %all-gather.5.cloned.1.call-done, bf16[8192,8192]{1,0:T(8,128)(2,1)} %param.19), kind=kOutput, calls=%fused_computation.107 | convolution fusion | flops 412484632576 | bytes 293601280 | tf_op jit(solution)/shard_map/bsd,df->bsf/dot_general | solution.py:71
  1365.0 50.6 %fusion.99 = u8[1024,8192]{1,0:T(8,128)(4,1)} fusion(f32[3,1024,8192]{2,1,0:T(8,128)} %get-tuple-element.82), kind=kLoop, calls=%fused_computation.108 | loop fusion | flops 192937984 | bytes 109051904
  1415.6 116.8 %convolution_bitcast_fusion = f32[3,4,256,8192]{3,2,0,1:T(8,128)} fusion(bf16[4,3,256,2048]{2,3,1,0:T(8,128)(2,1)} %get-tuple-element.42, bf16[2048,8192]{1,0:T(8,128)(2,1)} %param.18), kind=kOutput, calls=%fused_computation.92 | convolution fusion | flops 103079215104 | bytes 146800640 | tf_op jit(solution)/shard_map/nbqc,cd->bnqd/dot_general | solution.py:60
  1532.4 65.2 %copy.20 = f32[3,4,256,8192]{3,2,1,0:T(8,128)} copy(f32[3,4,256,8192]{3,2,0,1:T(8,128)} %convolution_bitcast_fusion) | data formatting | bytes 201326592 | tf_op jit(solution)/shard_map/nbqc,cd->bnqd/transpose | solution.py:60
  1597.6 228.9 %fusion.157 = bf16[3,1024,8192]{2,1,0:T(8,128)(2,1)} fusion(f32[3,1024,8192]{2,1,0:T(8,128)} %get-tuple-element.82, u8[1024,8192]{1,0:T(8,128)(4,1)} %get-tuple-element.81, u8[1024,8192]{1,0:T(8,128)(4,1)} %fusion.99), kind=kLoop, calls=%fused_computation.34.clone.clone.clone.clone.1 | loop fusion | flops 1761607680 | bytes 167772160 | tf_op jit(solution)/shard_map/bsf,fd->bsd/dot_general | solution.py:73
  1826.5 455.2 %bitcast_add_fusion = f32[3,1024,8192]{2,1,0:T(8,128)} fusion(f32[3,4,256,8192]{3,2,1,0:T(8,128)} %copy.20, bf16[8192,8192]{1,0:T(8,128)(2,1)} %param.20, bf16[3,1024,8192]{2,1,0:T(8,128)(2,1)} %fusion.157), kind=kOutput, calls=%fused_computation.40 | convolution fusion | flops 412342026240 | bytes 385875968 | tf_op jit(solution)/shard_map/bsf,fd->bsd/dot_general | solution.py:73
  2281.8 640.3 %reduce-scatter.2.cloned.1.call-done = f32[3,256,8192]{2,1,0:T(8,128)} async-done(((f32[3,1024,8192]{2,1,0:T(8,128)}), f32[3,256,8192]{2,1,0:T(8,128)}) %reduce-scatter.2.cloned.1.call-update) | async-done | bytes 25165840 | tf_op jit(solution)/shard_map/reduce_scatter | solution.py:74
  2922.1 17.2 fusion.95
  (49 shorter events, 37.2 us)
Async XLA Ops:
  6.5 327.7 %all-gather.3.cloned.1.call-start = ((), (), s32[]{:S(2)}) async-start(), calls=%async_computation.1 | async-start | bytes 62914560 | tf_op jit(solution)/shard_map/all_gather | solution.py:68
  36.8 828.1 %all-gather.5.cloned.1.call-start = ((), (), s32[]{:S(2)}) async-start(), calls=%async_computation.2 | async-start | bytes 62914560 | tf_op jit(solution)/shard_map/all_gather | solution.py:69
  37.5 2884.6 %reduce-scatter.2.cloned.1.call-start = ((), (), s32[]{:S(2)}) async-start(), calls=%async_computation.3 | async-start | bytes 125829120 | tf_op jit(solution)/shard_map/reduce_scatter | solution.py:74
  466.4 57.0 %copy-start = (f32[1024,64]{0,1:T(8,128)S(1)}, f32[1024,64]{0,1:T(8,128)}, u32[]{:S(2)}) copy-start(f32[1024,64]{0,1:T(8,128)} %get-tuple-element.79) | copy-start | bytes 786436
  466.4 57.0 %copy-start.1 = (f32[1024,64]{0,1:T(8,128)S(1)}, f32[1024,64]{0,1:T(8,128)}, u32[]{:S(2)}) copy-start(f32[1024,64]{0,1:T(8,128)} %get-tuple-element.80) | copy-start | bytes 786436
  485.1 40.7 %slice-start = ((s8[14155776]{0:T(1024)(128)(4,1)}), s8[4194304]{0:T(1024)(128)(4,1)S(1)}, s32[]{:S(2)}) async-start(s8[14155776]{0:T(1024)(128)(4,1)} %bitcast.92), calls=%async_computation.4 | async-start | bytes 8388608
  487.7 38.0 %slice-start.1 = ((s8[14155776]{0:T(1024)(128)(4,1)}), s8[4194304]{0:T(1024)(128)(4,1)S(1)}, s32[]{:S(2)}) async-start(s8[14155776]{0:T(1024)(128)(4,1)} %bitcast.92), calls=%async_computation.5 | async-start | bytes 8388608
  502.5 23.3 slice-start.2
  502.5 23.3 slice-start.3
Sparse Core Ops, SparseCore 0:
  36.9 297.3 all-gather.2
  335.8 294.4 all-gather.4
  2281.9 640.1 reduce-scatter.1
where the time goes:
time: 2950 us
  matrix products  1510 us (51%)
  waiting for transfers between devices  935 us (32%)
  other arithmetic  387 us (13%)
  local copies, waits for them, and re-layouts  97.1 us (3%)
    reduce_scatter x1, waiting for transfers between devices, local_layer(): lax.psum_scatter(attn_part + mlp_part, 'tp', scatter_dimension=1, tiled=T...  640 us
    dot_general x1, matrix products, local_layer(): jnp.einsum('bsd,df->bsf', mlp_in, w_up_part, preferred_element_type=jnp.f...  500 us
    dot_general x1, matrix products, local_layer(): jnp.einsum('bsf,fd->bsd', up_act, w_down_part, preferred_element_type=jnp...  455 us
    all_gather x1, waiting for transfers between devices, local_layer(): attn_in = lax.all_gather(normed_attn, 'tp', axis=1, tiled=True)  294 us
    dot_general x1, other arithmetic, local_layer(): jnp.einsum('bsf,fd->bsd', up_act, w_down_part, preferred_element_type=jnp...  229 us
    sub x4, matrix products, one_block(): exp_scores = jnp.exp(scores - jnp.max(scores, axis=-1, keepdims=True))  173 us
    dot_general x4, matrix products, one_block(): jnp.einsum('bkgqs,bskh->bqkgh', attn_probs, value_seq, preferred_element_...  133 us
    dot_general x1, matrix products, attention_branch(): jnp.einsum('bsd,dkc->bskc', normed, w_qkv_part, preferred_element_type=jn...  132 us
  transfers between devices with their start and end apart: 3, of which 2 were waited for; matrix products, arithmetic and copies ran while one was open for 18% of the time, Pallas kernels for 0%

commit v1 on v0

v1 whole, which is shorter than its diff:
```python
import functools

import jax
import jax.numpy as jnp
from jax import lax
from jax.experimental import pallas as pl
from jax.experimental.pallas import tpu as pltpu
from jax.sharding import PartitionSpec as P


BF16 = jnp.bfloat16
F32 = jnp.float32
VMEM_LIMIT = 63 * 2 ** 20
LOG2E = 1.4426950408889634


def params(**kw):
    return pltpu.CompilerParams(vmem_limit_bytes=VMEM_LIMIT, **kw)


def norm_kernel(slab, x_ref, ag_ref, ab_ref, mg_ref, mb_ref, a_ref, m_ref):
    def body(i, carry):
        rows = pl.ds(pl.multiple_of(i * slab, slab), slab)
        x = x_ref[rows, :].astype(F32)
        width = x.shape[-1]
        mean = jnp.sum(x, axis=-1, keepdims=True) * (1.0 / width)
        cen = x - mean
        var = jnp.sum(cen * cen, axis=-1, keepdims=True) * (1.0 / width)
        hat = cen * lax.rsqrt(var + 1e-5)
        a_ref[rows, :] = (hat * ag_ref[...] + ab_ref[...]).astype(BF16)
        m_ref[rows, :] = (hat * mg_ref[...] + mb_ref[...]).astype(BF16)
        return carry

    lax.fori_loop(0, x_ref.shape[0] // slab, body, 0)


def both_norms(x, ag, ab, mg, mb):
    rows, width = x.shape
    blk = 64
    vec = pl.BlockSpec((1, width), lambda i: (0, 0))
    row = pl.BlockSpec((blk, width), lambda i: (i, 0))
    return pl.pallas_call(
        functools.partial(norm_kernel, 16),
        grid=(rows // blk,),
        out_shape=(jax.ShapeDtypeStruct(x.shape, BF16),) * 2,
        in_specs=[row, vec, vec, vec, vec],
        out_specs=(row, row),
        compiler_params=params(),
        cost_estimate=pl.CostEstimate(flops=2 * 10 ** 10, bytes_accessed=6 * x.size, transcendentals=0),
        name="norms",
    )(x, ag, ab, mg, mb)


def up_kernel(sub, x_ref, w_ref, o_ref):
    def body(i, carry):
        rows = pl.ds(pl.multiple_of(i * sub, sub), sub)
        pre = jnp.dot(x_ref[rows, :], w_ref[...], preferred_element_type=F32)
        o_ref[rows, :] = (0.5 * pre * (1.0 + lax.erf(pre * (2.0 ** -0.5)))).astype(BF16)
        return carry

    lax.fori_loop(0, x_ref.shape[0] // sub, body, 0)


def up_gelu(x, w):
    rows, depth = x.shape
    cols = w.shape[1]
    bn = 512
    return pl.pallas_call(
        functools.partial(up_kernel, 384),
        grid=(cols // bn,),
        out_shape=jax.ShapeDtypeStruct((rows, cols), BF16),
        in_specs=[
            pl.BlockSpec((rows, depth), lambda j: (0, 0), pipeline_mode=pl.Buffered(1)),
            pl.BlockSpec((depth, bn), lambda j: (0, j)),
        ],
        out_specs=pl.BlockSpec((rows, bn), lambda j: (0, j)),
        compiler_params=params(),
        cost_estimate=pl.CostEstimate(flops=2 * rows * depth * cols, bytes_accessed=2 * (x.size + w.size + rows * cols), transcendentals=rows * cols),
        name="up_gelu",
    )(x, w)


def rotate(vals, cos, sin, low):
    turned = jnp.where(low, pltpu.roll(vals, 96, 1), pltpu.roll(vals, 32, 1))
    return vals * cos + turned * sin


def attn_kernel(blk, scale, tp_ref, r0, r1, r2, r3, cq_ref, sq_ref, ck_ref, sk_ref, o_ref, q_ref, kt_ref, v_ref):
    t = pl.program_id(2)
    slots = (r0, r1, r2, r3)
    pairs = o_ref.shape[-1] // 128
    lane = lax.broadcasted_iota(jnp.int32, (blk, 128), 1)
    low = lax.rem(lane, 64) < 32
    first = lane < 64

    @pl.when(t == 0)
    def _():
        for k, ref in enumerate(slots):
            at = pl.multiple_of((tp_ref[0] ^ k) * blk, blk)
            rows = pl.ds(at, blk)
            kv = rotate(ref[0, 0, :, pairs * 128:].astype(F32), ck_ref[rows, :], sk_ref[rows, :], low)
            kv = kv.astype(BF16).astype(F32)
            swapped = pltpu.roll(kv, 64, 1)
            kt_ref[0, :, rows] = jnp.transpose(jnp.where(first, kv, 0.0)).astype(BF16)
            kt_ref[1, :, rows] = jnp.transpose(jnp.where(first, 0.0, swapped)).astype(BF16)
            v_ref[0, rows, :] = jnp.where(first, swapped, 0.0).astype(BF16)
            v_ref[1, rows, :] = jnp.where(first, 0.0, kv).astype(BF16)

    for k, ref in enumerate(slots):
        @pl.when((t ^ tp_ref[0]) == k)
        def _(ref=ref):
            for p in range(pairs):
                cols = slice(p * 128, (p + 1) * 128)
                q_ref[:, cols] = rotate(ref[0, 0, :, cols].astype(F32), cq_ref[...], sq_ref[...], low).astype(BF16)

    allowed = lax.broadcasted_iota(jnp.int32, (blk, blk), 1) <= lax.broadcasted_iota(jnp.int32, (blk, blk), 0)

    for tt in range(4):
        @pl.when(t == tt)
        def _(tt=tt):
            keys = (tt + 1) * blk

            def body(p, carry):
                cols = pl.ds(pl.multiple_of(p * 128, 128), 128)
                q = q_ref[:, cols]
                ctx = None
                for e in range(2):
                    s = jnp.dot(q, kt_ref[e, :, :keys], preferred_element_type=F32)
                    diag = jnp.where(allowed, s[:, keys - blk:], -1e30)
                    s = jnp.concatenate([s[:, :keys - blk], diag], axis=1) if tt else diag
                    top = jnp.max(s, axis=-1, keepdims=True)
                    ex = jnp.exp2((s - top) * (scale * LOG2E))
                    prob = (ex * (1.0 / jnp.sum(ex, axis=-1, keepdims=True))).astype(BF16)
                    part = jnp.dot(prob, v_ref[e, :keys, :], preferred_element_type=F32)
                    ctx = part if ctx is None else ctx + part
                o_ref[0, :, cols] = ctx.astype(BF16)
                return carry

            lax.fori_loop(0, pairs, body, 0)


def attention(qkv, my, positions):
    slots = len(qkv)
    batch, groups, blk, cols = qkv[0].shape
    head = 64
    qcols = cols - 2 * head
    inv_freq = 10000.0 ** (-2.0 * jnp.arange(head // 2, dtype=F32) / head)
    ang = positions.astype(F32)[:, None] * inv_freq[None, :]
    cos, sin = jnp.cos(ang), jnp.sin(ang)
    ones, zeros = jnp.ones_like(cos), jnp.zeros_like(sin)
    cq = jnp.concatenate([cos, cos, cos, cos], axis=1)
    sq = jnp.concatenate([-sin, sin, -sin, sin], axis=1)
    ck = jnp.concatenate([cos, cos, ones, ones], axis=1)
    sk = jnp.concatenate([-sin, sin, zeros, zeros], axis=1)
    tokens = slots * blk
    tab = pl.BlockSpec((blk, 128), lambda b, g, t, tp: (t, 0))
    full = pl.BlockSpec((tokens, 128), lambda b, g, t, tp: (0, 0))
    part = pl.BlockSpec((1, 1, blk, cols), lambda b, g, t, tp: (b, g, 0, 0))
    work = batch * groups * (qcols // head) * tokens * tokens // 2
    return pl.pallas_call(
        functools.partial(attn_kernel, blk, head ** -0.5),
        grid_spec=pltpu.PrefetchScalarGridSpec(
            num_scalar_prefetch=1,
            grid=(batch, groups, slots),
            in_specs=[part] * slots + [tab, tab, full, full],
            out_specs=pl.BlockSpec((1, blk, qcols), lambda b, g, t, tp: (tp[0] ^ t, b, g)),
            scratch_shapes=[pltpu.VMEM((blk, qcols), BF16), pltpu.VMEM((2, 128, tokens), BF16), pltpu.VMEM((2, tokens, 128), BF16)],
        ),
        out_shape=jax.ShapeDtypeStruct((slots, batch * blk, groups * qcols), BF16),
        compiler_params=params(),
        cost_estimate=pl.CostEstimate(flops=1000 * work, bytes_accessed=8 * qkv[0].size, transcendentals=work),
        name="attention",
    )(my, *qkv, cq, sq, ck, sk)


def down_kernel(sub, n_add, h_ref, c_ref, wd_ref, wo_ref, *refs):
    o_ref = refs[-1]

    def body(i, carry):
        rows = pl.ds(pl.multiple_of(i * sub, sub), sub)
        acc = jnp.dot(h_ref[rows, :], wd_ref[...], preferred_element_type=F32)
        acc += jnp.dot(c_ref[0, rows, :], wo_ref[...], preferred_element_type=F32)
        for add in refs[:n_add]:
            acc += add[rows, :].astype(F32)
        o_ref[rows, :] = acc.astype(BF16)
        return carry

    lax.fori_loop(0, h_ref.shape[0] // sub, body, 0)


def down(h, ctx, slot, wd, wo, half, adds=(), into=None, wide=False):
    rows, depth = h.shape
    width = wd.shape[1]
    bn = 512
    n = width // 2 // bn
    off = half * n

    def cols_spec(is_wide):
        return pl.BlockSpec((rows, bn), (lambda j: (0, j + off)) if is_wide else (lambda j: (0, j)))

    in_specs = [
        pl.BlockSpec((rows, depth), lambda j: (0, 0), pipeline_mode=pl.Buffered(1)),
        pl.BlockSpec((1, rows, ctx.shape[2]), lambda j: (slot, 0, 0), pipeline_mode=pl.Buffered(1)),
        pl.BlockSpec((depth, bn), lambda j: (0, j + off)),
        pl.BlockSpec((wo.shape[0], bn), lambda j: (0, j + off)),
    ] + [cols_spec(w) for _, w in adds]
    args = [h, ctx, wd, wo] + [a for a, _ in adds]
    alias = {}
    if into is not None:
        in_specs.append(pl.BlockSpec(memory_space=pl.ANY))
        alias = {len(args): 0}
        args.append(into)
    return pl.pallas_call(
        functools.partial(down_kernel, 384, len(adds)),
        grid=(n,),
        out_shape=jax.ShapeDtypeStruct((rows, width if wide else width // 2), BF16),
        in_specs=in_specs,
        out_specs=cols_spec(wide),
        input_output_aliases=alias,
        compiler_params=params(),
        cost_estimate=pl.CostEstimate(flops=rows * (depth + wo.shape[0]) * width, bytes_accessed=depth * width + 4 * rows * width, transcendentals=0),
        name="down",
    )(*args)


def solution(mesh):
    def local_layer(hidden, attn_gain, attn_bias, mlp_gain, mlp_bias, w_qkv, w_out, w_up, w_down, positions):
        batch, blk, width = hidden.shape
        rows = batch * blk
        x = hidden.reshape(rows, width)
        vecs = [v.reshape(1, width) for v in (attn_gain, attn_bias, mlp_gain, mlp_bias)]
        mate = functools.partial(lax.ppermute, axis_name='tp', perm=[(i, i ^ 1) for i in range(4)])
        over = functools.partial(lax.ppermute, axis_name='tp', perm=[(i, i ^ 2) for i in range(4)])

        def qkv_of(a):
            return jnp.einsum('bsd,dkc->bksc', a.reshape(batch, blk, width), w_qkv, preferred_element_type=F32).astype(BF16)

        def after(val, dep):
            return lax.optimization_barrier((val, dep))[0]

        x2 = over(x)
        a0, m0 = both_norms(x, *vecs)
        m1 = mate(m0)
        a1 = mate(a0)
        h0 = up_gelu(m0, w_up)
        q0 = qkv_of(after(a0, h0))
        h1 = up_gelu(after(m1, q0), w_up)
        q1 = qkv_of(after(a1, h1))
        a2, m2 = both_norms(after(x2, q1), *vecs)
        m3 = mate(m2)
        a3 = mate(a2)
        h2 = up_gelu(m2, w_up)
        q2 = qkv_of(after(a2, h2))
        h3 = up_gelu(after(m3, q2), w_up)
        q3 = qkv_of(after(a3, h3))

        my = lax.axis_index('tp').astype(jnp.int32).reshape(1)
        ctx = attention([q0, q1, q2, q3], my, positions)

        last, got = h3, {}
        hs = (h0, h1, h2, h3)
        out = None
        for slot in (3, 2, 1, 0):
            for s in range(2):
                adds = ()
                if slot == 2:
                    adds = ((got[3, s], False),)
                if slot == 0:
                    adds = ((got[1, s], False), (got[2, s], False), (x, True))
                last = down(after(hs[slot], last), ctx, slot, w_down, w_out, s, adds=adds, into=out, wide=slot == 0)
                if slot == 0:
                    out = last
                else:
                    got[slot, s] = (over if slot == 2 else mate)(last)
        return out.reshape(batch, blk, width)

    return jax.shard_map(local_layer, mesh=mesh, in_specs=(P('dp', 'tp', None), P(), P(), P(), P(), P(None, 'tp', None), P('tp', None), P(None, 'tp'), P('tp', None), P()), out_specs=P('dp', 'tp', None), check_vma=False)
```

time: 2950 us -> 1630 us (0.55)
  matrix products: 1510 us -> 159 us
  Pallas kernels: 0 us -> 1340 us
  waiting for transfers between devices: 935 us -> 114 us
  other arithmetic: 387 us -> 4.1 us
  local copies, waits for them, and re-layouts: 97.1 us -> 0.16 us
    pallas_call x0 -> x15, Pallas kernels: none -> 1340 us  [the longest x8 624 us: down(): pl.pallas_call(functools.partial(down_kernel, 384, len(adds)), grid=(n,),...]
    dot_general x8 -> x4, matrix products: 1340 us -> 159 us  [qkv_of(): jnp.einsum('bsd,dkc->bksc', a.reshape(batch, blk, width), w_qkv, preferre...]
    reduce_scatter x1 -> x0, waiting for transfers between devices: 640 us -> none  [local_layer(): lax.psum_scatter(attn_part + mlp_part, 'tp', scatter_dimension=1, tiled=T...]
    all_gather x2 -> x0, waiting for transfers between devices: 294 us -> none  [the longest x1 294 us: local_layer(): attn_in = lax.all_gather(normed_attn, 'tp', axis=1, tiled=True)]
    dot_general x1 -> x0, other arithmetic: 229 us -> none  [local_layer(): jnp.einsum('bsf,fd->bsd', up_act, w_down_part, preferred_element_type=jnp...]
    sub x4 -> x0, matrix products: 173 us -> none  [one_block(): exp_scores = jnp.exp(scores - jnp.max(scores, axis=-1, keepdims=True))]
    ppermute x0 -> x11, waiting for transfers between devices: none -> 114 us  [the longest x6 114 us: local_layer(): got[slot, s] = (over if slot == 2 else mate)(last)]
    convert_element_type x6 -> x1, other arithmetic: 66.1 us -> 0.01 us  [attention(): ang = positions.astype(F32)[:, None] * inv_freq[None, :]]
  transfers between devices with their start and end apart: 3 -> 11, of which waited for: 2 -> 2; matrix products, arithmetic and copies ran while one was open for 18% -> 8% of each run, Pallas kernels for 0% -> 50%
where the time goes in v1:
time: 1630 us
  Pallas kernels  1340 us (82%)
  matrix products  159 us (10%)
  waiting for transfers between devices  114 us (7%)
    pallas_call x8, Pallas kernels, down(): pl.pallas_call(functools.partial(down_kernel, 384, len(adds)), grid=(n,),...  624 us
    pallas_call x4, Pallas kernels, up_gelu(): pl.pallas_call(functools.partial(up_kernel, 384), grid=(cols // bn,), out...  474 us
    pallas_call x1, Pallas kernels, attention(): pl.pallas_call(functools.partial(attn_kernel, blk, head ** (-0.5)), grid_...  186 us
    dot_general x4, matrix products, qkv_of(): jnp.einsum('bsd,dkc->bksc', a.reshape(batch, blk, width), w_qkv, preferre...  159 us
    ppermute x6, waiting for transfers between devices, local_layer(): got[slot, s] = (over if slot == 2 else mate)(last)  114 us
    pallas_call x2, Pallas kernels, both_norms(): pl.pallas_call(functools.partial(norm_kernel, 16), grid=(rows // blk,), o...  58.4 us
  transfers between devices with their start and end apart: 11, of which 2 were waited for; matrix products, arithmetic and copies ran while one was open for 8% of the time, Pallas kernels for 50%

profile of v1, /device:TPU:0, one launch (start us, length us, event | category | flops | bytes accessed | tf_op | source)
XLA Modules:
  0.0 1627.3 jit_solution(13805853906114809633)
XLA Ops:
  0.0 3.3 collective-permute-start.1
  3.3 29.3 %norms.2 = (bf16[768,8192]{1,0:T(8,128)(2,1)}, bf16[768,8192]{1,0:T(8,128)(2,1)}) custom-call(bf16[768,8192]{1,0:T(8,128)(2,1)} %bitcast.68, f32[1,8192]{1,0:T(1,128)} %bitcast.73, f32[1,8192]{1,0:T(1,128)} %bitcast.75, f32[1,8192]{1,0:T(1,128)} %bitcast.77, f32[1,8192]{1,0:T(1,128)} %bitcast.79), custom_call_target="tpu_custom_call" | custom-call | flops 20000000000 | bytes 37748736 | tf_op jit(solution)/shard_map/norms/pallas_call | solution.py:42
  33.1 118.6 %up_gelu.4.h_ref = bf16[768,8192]{1,0:T(8,128)(2,1)} custom-call(bf16[768,8192]{1,0:T(8,128)(2,1)} %get-tuple-element.24.x_ref, bf16[8192,8192]{1,0:T(8,128)(2,1)} %w_ref.7), custom_call_target="tpu_custom_call" | custom-call | flops 103079215104 | bytes 159383552 | tf_op jit(solution)/shard_map/up_gelu/pallas_call | solution.py:68
  151.9 1.9 fusion.38
  153.8 2.2 fusion.36
  156.0 40.0 %fusion.33.r0 = bf16[3,2,256,1152]{3,2,1,0:T(8,128)(2,1)} fusion(bf16[3,256,8192,1]{2,1,3,0:T(8,128)(2,1)} %bitcast.71, bf16[8192,2,1152]{2,1,0:T(2,128)(2,1)} %param.15), kind=kOutput, calls=%fused_computation.19 | convolution fusion | flops 28992798720 | bytes 53870592 | tf_op jit(solution)/shard_map/bsd,dkc->bksc/dot_general | solution.py:236
  196.0 118.6 %up_gelu.5.h_ref = bf16[768,8192]{1,0:T(8,128)(2,1)} custom-call(bf16[768,8192]{1,0:T(8,128)(2,1)} %collective-permute-done.x_ref, bf16[8192,8192]{1,0:T(8,128)(2,1)} %w_ref.7), custom_call_target="tpu_custom_call" | custom-call | flops 103079215104 | bytes 159383552 | tf_op jit(solution)/shard_map/up_gelu/pallas_call | solution.py:68
  314.6 39.6 %fusion.30.r1 = bf16[3,2,256,1152]{3,2,1,0:T(8,128)(2,1)} fusion(bf16[3,256,8192,1]{2,1,3,0:T(8,128)(2,1)} %bitcast.12, bf16[8192,2,1152]{2,1,0:T(2,128)(2,1)} %param.15), kind=kOutput, calls=%fused_computation.18 | convolution fusion | flops 28992798720 | bytes 53870592 | tf_op jit(solution)/shard_map/bsd,dkc->bksc/dot_general | solution.py:236
  354.2 29.2 %norms.3 = (bf16[768,8192]{1,0:T(8,128)(2,1)}, bf16[768,8192]{1,0:T(8,128)(2,1)}) custom-call(bf16[768,8192]{1,0:T(8,128)(2,1)} %collective-permute-done.1.x_ref, f32[1,8192]{1,0:T(1,128)} %bitcast.74, f32[1,8192]{1,0:T(1,128)} %bitcast.76, f32[1,8192]{1,0:T(1,128)} %bitcast.78, f32[1,8192]{1,0:T(1,128)} %bitcast.80), custom_call_target="tpu_custom_call" | custom-call | flops 20000000000 | bytes 37748736 | tf_op jit(solution)/shard_map/norms/pallas_call | solution.py:42
  383.9 118.5 %up_gelu.6.h_ref = bf16[768,8192]{1,0:T(8,128)(2,1)} custom-call(bf16[768,8192]{1,0:T(8,128)(2,1)} %get-tuple-element.30.x_ref, bf16[8192,8192]{1,0:T(8,128)(2,1)} %w_ref.7), custom_call_target="tpu_custom_call" | custom-call | flops 103079215104 | bytes 159383552 | tf_op jit(solution)/shard_map/up_gelu/pallas_call | solution.py:68
  502.4 39.7 %fusion.27.r2 = bf16[3,2,256,1152]{3,2,1,0:T(8,128)(2,1)} fusion(bf16[3,256,8192,1]{2,1,3,0:T(8,128)(2,1)} %bitcast.72, bf16[8192,2,1152]{2,1,0:T(2,128)(2,1)} %param.15), kind=kOutput, calls=%fused_computation.17 | convolution fusion | flops 28992798720 | bytes 53870592 | tf_op jit(solution)/shard_map/bsd,dkc->bksc/dot_general | solution.py:236
  542.2 118.6 %up_gelu.7.h_ref = bf16[768,8192]{1,0:T(8,128)(2,1)} custom-call(bf16[768,8192]{1,0:T(8,128)(2,1)} %collective-permute-done.3.x_ref, bf16[8192,8192]{1,0:T(8,128)(2,1)} %w_ref.7), custom_call_target="tpu_custom_call" | custom-call | flops 103079215104 | bytes 159383552 | tf_op jit(solution)/shard_map/up_gelu/pallas_call | solution.py:68
  660.8 39.8 %fusion.24.r3 = bf16[3,2,256,1152]{3,2,1,0:T(8,128)(2,1)} fusion(bf16[3,256,8192,1]{2,1,3,0:T(8,128)(2,1)} %bitcast.23, bf16[8192,2,1152]{2,1,0:T(2,128)(2,1)} %param.15), kind=kOutput, calls=%fused_computation.16 | convolution fusion | flops 28992798720 | bytes 53870592 | tf_op jit(solution)/shard_map/bsd,dkc->bksc/dot_general | solution.py:236
  700.6 185.9 %attention.1.c_ref = bf16[4,768,2048]{2,1,0:T(8,128)(2,1)} custom-call(s32[1]{0:T(128)} %bitcast.20.tp_ref, bf16[3,2,256,1152]{3,2,1,0:T(8,128)(2,1)} %fusion.33.r0, bf16[3,2,256,1152]{3,2,1,0:T(8,128)(2,1)} %fusion.30.r1, bf16[3,2,256,1152]{3,2,1,0:T(8,128)(2,1)} %fusion.27.r2, bf16[3,2,256,1152]{3,2,1,0:T(8,128)(2,1)} %fusion.24.r3, ...), custom_call_target="tpu_custom_call" | custom-call | flops 50331648000 | bytes 14155776 | tf_op jit(solution)/shard_map/attention/pallas_call | solution.py:160
  886.4 77.0 %down.8 = bf16[768,4096]{1,0:T(8,128)(2,1)} custom-call(bf16[768,8192]{1,0:T(8,128)(2,1)} %up_gelu.7.h_ref, bf16[4,768,2048]{2,1,0:T(8,128)(2,1)} %attention.1.c_ref, bf16[8192,8192]{1,0:T(8,128)(2,1)} %wd_ref.15, bf16[2048,8192]{1,0:T(8,128)(2,1)} %wo_ref.15), custom_call_target="tpu_custom_call" | custom-call | flops 64424509440 | bytes 92274688 | tf_op jit(solution)/shard_map/down/pallas_call | solution.py:213
  963.4 77.0 %down.9 = bf16[768,4096]{1,0:T(8,128)(2,1)} custom-call(bf16[768,8192]{1,0:T(8,128)(2,1)} %up_gelu.7.h_ref, bf16[4,768,2048]{2,1,0:T(8,128)(2,1)} %attention.1.c_ref, bf16[8192,8192]{1,0:T(8,128)(2,1)} %wd_ref.15, bf16[2048,8192]{1,0:T(8,128)(2,1)} %wo_ref.15), custom_call_target="tpu_custom_call" | custom-call | flops 64424509440 | bytes 92274688 | tf_op jit(solution)/shard_map/down/pallas_call | solution.py:213
  1040.9 77.9 %down.10 = bf16[768,4096]{1,0:T(8,128)(2,1)} custom-call(bf16[768,8192]{1,0:T(8,128)(2,1)} %up_gelu.6.h_ref, bf16[4,768,2048]{2,1,0:T(8,128)(2,1)} %attention.1.c_ref, bf16[8192,8192]{1,0:T(8,128)(2,1)} %wd_ref.15, bf16[2048,8192]{1,0:T(8,128)(2,1)} %wo_ref.15, bf16[768,4096]{1,0:T(8,128)(2,1)} %collective-permute-done.5.refs_0_), custom_call_target="tpu_custom_call" | custom-call | flops 64424509440 | bytes 92274688 | tf_op jit(solution)/shard_map/down/pallas_call | solution.py:213
  1118.8 78.3 %down.11 = bf16[768,4096]{1,0:T(8,128)(2,1)} custom-call(bf16[768,8192]{1,0:T(8,128)(2,1)} %up_gelu.6.h_ref, bf16[4,768,2048]{2,1,0:T(8,128)(2,1)} %attention.1.c_ref, bf16[8192,8192]{1,0:T(8,128)(2,1)} %wd_ref.15, bf16[2048,8192]{1,0:T(8,128)(2,1)} %wo_ref.15, bf16[768,4096]{1,0:T(8,128)(2,1)} %collective-permute-done.6.refs_0_), custom_call_target="tpu_custom_call" | custom-call | flops 64424509440 | bytes 92274688 | tf_op jit(solution)/shard_map/down/pallas_call | solution.py:213
  1197.1 76.9 %down.12 = bf16[768,4096]{1,0:T(8,128)(2,1)} custom-call(bf16[768,8192]{1,0:T(8,128)(2,1)} %up_gelu.5.h_ref, bf16[4,768,2048]{2,1,0:T(8,128)(2,1)} %attention.1.c_ref, bf16[8192,8192]{1,0:T(8,128)(2,1)} %wd_ref.15, bf16[2048,8192]{1,0:T(8,128)(2,1)} %wo_ref.15), custom_call_target="tpu_custom_call" | custom-call | flops 64424509440 | bytes 92274688 | tf_op jit(solution)/shard_map/down/pallas_call | solution.py:213
  1274.1 77.1 %down.13 = bf16[768,4096]{1,0:T(8,128)(2,1)} custom-call(bf16[768,8192]{1,0:T(8,128)(2,1)} %up_gelu.5.h_ref, bf16[4,768,2048]{2,1,0:T(8,128)(2,1)} %attention.1.c_ref, bf16[8192,8192]{1,0:T(8,128)(2,1)} %wd_ref.15, bf16[2048,8192]{1,0:T(8,128)(2,1)} %wo_ref.15), custom_call_target="tpu_custom_call" | custom-call | flops 64424509440 | bytes 92274688 | tf_op jit(solution)/shard_map/down/pallas_call | solution.py:213
  1353.4 59.4 %collective-permute-done.8.refs_1_ = bf16[768,4096]{1,0:T(8,128)(2,1)} collective-permute-done((bf16[768,4096]{1,0:T(8,128)(2,1)}, bf16[768,4096]{1,0:T(8,128)(2,1)}, u32[]{:S(2)}, u32[]{:S(2)}) %collective-permute-start.8) | collective-permute-done | bytes 6291488 | tf_op jit(solution)/shard_map/ppermute | solution.py:274
  1412.8 79.8 %down.14.refs_3_ = bf16[768,8192]{1,0:T(8,128)(2,1)} custom-call(bf16[768,8192]{1,0:T(8,128)(2,1)} %up_gelu.4.h_ref, bf16[4,768,2048]{2,1,0:T(8,128)(2,1)} %attention.1.c_ref, bf16[8192,8192]{1,0:T(8,128)(2,1)} %wd_ref.15, bf16[2048,8192]{1,0:T(8,128)(2,1)} %wo_ref.15, bf16[768,4096]{1,0:T(8,128)(2,1)} %collective-permute-done.7.refs_0_, ...), custom_call_target="tpu_custom_call" | custom-call | flops 64424509440 | bytes 92274688 | tf_op jit(solution)/shard_map/down/pallas_call | solution.py:213
  1492.6 54.6 %collective-permute-done.10.refs_1_ = bf16[768,4096]{1,0:T(8,128)(2,1)} collective-permute-done((bf16[768,4096]{1,0:T(8,128)(2,1)}, bf16[768,4096]{1,0:T(8,128)(2,1)}, u32[]{:S(2)}, u32[]{:S(2)}) %collective-permute-start.10) | collective-permute-done | bytes 6291488 | tf_op jit(solution)/shard_map/ppermute | solution.py:274
  1547.1 80.0 %down.15 = bf16[768,8192]{1,0:T(8,128)(2,1)} custom-call(bf16[768,8192]{1,0:T(8,128)(2,1)} %up_gelu.4.h_ref, bf16[4,768,2048]{2,1,0:T(8,128)(2,1)} %attention.1.c_ref, bf16[8192,8192]{1,0:T(8,128)(2,1)} %wd_ref.15, bf16[2048,8192]{1,0:T(8,128)(2,1)} %wo_ref.15, bf16[768,4096]{1,0:T(8,128)(2,1)} %collective-permute-done.9.refs_0_, ...), custom_call_target="tpu_custom_call", output_to_operand_aliasing={{}: (7, {})} | custom-call | flops 64424509440 | bytes 92274688 | tf_op jit(solution)/shard_map/down/pallas_call | solution.py:213
  (27 shorter events, 4.0 us)
Async XLA Ops:
  0.0 354.2 %collective-permute-start.1 = (bf16[768,8192]{1,0:T(8,128)(2,1)}, bf16[768,8192]{1,0:T(8,128)(2,1)}, u32[]{:S(2)}, u32[]{:S(2)}) collective-permute-start(bf16[768,8192]{1,0:T(8,128)(2,1)} %bitcast.67), channel_id=1, source_target_pairs={{0,2},{1,3},{2,0},{3,1},{4,6},{5,7},{6,4},{7,5}} | collective-permute-start | bytes 37748744 | tf_op jit(solution)/shard_map/ppermute | solution.py:241
  32.6 163.4 %collective-permute-start = (bf16[768,8192]{1,0:T(8,128)(2,1)}, bf16[768,8192]{1,0:T(8,128)(2,1)}, u32[]{:S(2)}, u32[]{:S(2)}) collective-permute-start(bf16[768,8192]{1,0:T(8,128)(2,1)} %get-tuple-element.24.x_ref), channel_id=1, source_target_pairs={{0,1},{1,0},{2,3},{3,2},{4,5},{5,4},{6,7},{7,6}} | collective-permute-start | bytes 37748744 | tf_op jit(solution)/shard_map/ppermute | solution.py:243
  32.6 282.0 %collective-permute-start.2 = (bf16[768,8192]{1,0:T(8,128)(2,1)}, bf16[768,8192]{1,0:T(8,128)(2,1)}, u32[]{:S(2)}, u32[]{:S(2)}) collective-permute-start(bf16[768,8192]{1,0:T(8,128)(2,1)} %get-tuple-element.26), channel_id=1, source_target_pairs={{0,1},{1,0},{2,3},{3,2},{4,5},{5,4},{6,7},{7,6}} | collective-permute-start | bytes 37748744 | tf_op jit(solution)/shard_map/ppermute | solution.py:244
  33.1 118.6 %copy-start = (s32[1024]{0:T(1024)S(1)}, s32[1024]{0:T(1024)}, u32[]{:S(2)}) copy-start(s32[1024]{0:T(1024)} %param.19) | copy-start | bytes 12292
  383.4 158.8 %collective-permute-start.3 = (bf16[768,8192]{1,0:T(8,128)(2,1)}, bf16[768,8192]{1,0:T(8,128)(2,1)}, u32[]{:S(2)}, u32[]{:S(2)}) collective-permute-start(bf16[768,8192]{1,0:T(8,128)(2,1)} %get-tuple-element.30.x_ref), channel_id=1, source_target_pairs={{0,1},{1,0},{2,3},{3,2},{4,5},{5,4},{6,7},{7,6}} | collective-permute-start | bytes 37748744 | tf_op jit(solution)/shard_map/ppermute | solution.py:250
  383.4 277.4 %collective-permute-start.4 = (bf16[768,8192]{1,0:T(8,128)(2,1)}, bf16[768,8192]{1,0:T(8,128)(2,1)}, u32[]{:S(2)}, u32[]{:S(2)}) collective-permute-start(bf16[768,8192]{1,0:T(8,128)(2,1)} %get-tuple-element.32), channel_id=1, source_target_pairs={{0,1},{1,0},{2,3},{3,2},{4,5},{5,4},{6,7},{7,6}} | collective-permute-start | bytes 37748744 | tf_op jit(solution)/shard_map/ppermute | solution.py:251
  963.4 77.5 %collective-permute-start.5 = (bf16[768,4096]{1,0:T(8,128)(2,1)}, bf16[768,4096]{1,0:T(8,128)(2,1)}, u32[]{:S(2)}, u32[]{:S(2)}) collective-permute-start(bf16[768,4096]{1,0:T(8,128)(2,1)} %down.8), channel_id=1, source_target_pairs={{0,1},{1,0},{2,3},{3,2},{4,5},{5,4},{6,7},{7,6}} | collective-permute-start | bytes 18874376 | tf_op jit(solution)/shard_map/ppermute | solution.py:274
  1040.4 78.4 %collective-permute-start.6 = (bf16[768,4096]{1,0:T(8,128)(2,1)}, bf16[768,4096]{1,0:T(8,128)(2,1)}, u32[]{:S(2)}, u32[]{:S(2)}) collective-permute-start(bf16[768,4096]{1,0:T(8,128)(2,1)} %down.9), channel_id=1, source_target_pairs={{0,1},{1,0},{2,3},{3,2},{4,5},{5,4},{6,7},{7,6}} | collective-permute-start | bytes 18874376 | tf_op jit(solution)/shard_map/ppermute | solution.py:274
  1274.1 79.4 %collective-permute-start.7 = (bf16[768,4096]{1,0:T(8,128)(2,1)}, bf16[768,4096]{1,0:T(8,128)(2,1)}, u32[]{:S(2)}, u32[]{:S(2)}) collective-permute-start(bf16[768,4096]{1,0:T(8,128)(2,1)} %down.12), channel_id=1, source_target_pairs={{0,1},{1,0},{2,3},{3,2},{4,5},{5,4},{6,7},{7,6}} | collective-permute-start | bytes 18874376 | tf_op jit(solution)/shard_map/ppermute | solution.py:274
  1274.1 138.7 %collective-permute-start.8 = (bf16[768,4096]{1,0:T(8,128)(2,1)}, bf16[768,4096]{1,0:T(8,128)(2,1)}, u32[]{:S(2)}, u32[]{:S(2)}) collective-permute-start(bf16[768,4096]{1,0:T(8,128)(2,1)} %down.10), channel_id=1, source_target_pairs={{0,2},{1,3},{2,0},{3,1},{4,6},{5,7},{6,4},{7,5}} | collective-permute-start | bytes 18874376 | tf_op jit(solution)/shard_map/ppermute | solution.py:274
  1351.2 141.3 %collective-permute-start.9 = (bf16[768,4096]{1,0:T(8,128)(2,1)}, bf16[768,4096]{1,0:T(8,128)(2,1)}, u32[]{:S(2)}, u32[]{:S(2)}) collective-permute-start(bf16[768,4096]{1,0:T(8,128)(2,1)} %down.13), channel_id=1, source_target_pairs={{0,1},{1,0},{2,3},{3,2},{4,5},{5,4},{6,7},{7,6}} | collective-permute-start | bytes 18874376 | tf_op jit(solution)/shard_map/ppermute | solution.py:274
  1351.7 195.4 %collective-permute-start.10 = (bf16[768,4096]{1,0:T(8,128)(2,1)}, bf16[768,4096]{1,0:T(8,128)(2,1)}, u32[]{:S(2)}, u32[]{:S(2)}) collective-permute-start(bf16[768,4096]{1,0:T(8,128)(2,1)} %down.11), channel_id=1, source_target_pairs={{0,2},{1,3},{2,0},{3,1},{4,6},{5,7},{6,4},{7,5}} | collective-permute-start | bytes 18874376 | tf_op jit(solution)/shard_map/ppermute | solution.py:274

commit v2 on v1

--- a/solution.py
+++ b/solution.py
@@ -18,66 +18,128 @@
     return pltpu.CompilerParams(vmem_limit_bytes=VMEM_LIMIT, **kw)
 
 
-def norm_kernel(slab, x_ref, ag_ref, ab_ref, mg_ref, mb_ref, a_ref, m_ref):
-    def body(i, carry):
-        rows = pl.ds(pl.multiple_of(i * slab, slab), slab)
-        x = x_ref[rows, :].astype(F32)
-        width = x.shape[-1]
-        mean = jnp.sum(x, axis=-1, keepdims=True) * (1.0 / width)
-        cen = x - mean
-        var = jnp.sum(cen * cen, axis=-1, keepdims=True) * (1.0 / width)
-        hat = cen * lax.rsqrt(var + 1e-5)
-        a_ref[rows, :] = (hat * ag_ref[...] + ab_ref[...]).astype(BF16)
-        m_ref[rows, :] = (hat * mg_ref[...] + mb_ref[...]).astype(BF16)
+def norm_kernel(blk, step, x_ref, ag_ref, ab_ref, mg_ref, mb_ref, a_ref, m_ref, mean_ref, rstd_ref):
+    rows, width = x_ref.shape
+
+    def stats(i, carry):
+        at = pl.ds(pl.multiple_of(i * blk, blk), blk)
+
+        def piece(k):
+            return x_ref[at, pl.ds(pl.multiple_of(k * step, step), step)].astype(F32)
+
+        zero = jnp.zeros((blk, step), F32)
+        total = lax.fori_loop(0, width // step, lambda k, acc: acc + piece(k), zero, unroll=4)
+        mean = jnp.sum(total, axis=-1, keepdims=True) * (1.0 / width)
+
+        def square(k, acc):
+            cen = piece(k) - mean
+            return acc + cen * cen
+
+        total = lax.fori_loop(0, width // step, square, zero, unroll=4)
+        rstd = lax.rsqrt(jnp.sum(total, axis=-1, keepdims=True) * (1.0 / width) + 1e-5)
+        mean_ref[at, :] = jnp.broadcast_to(mean, (blk, 128))
+        rstd_ref[at, :] = jnp.broadcast_to(rstd, (blk, 128))
         return carry
 
-    lax.fori_loop(0, x_ref.shape[0] // slab, body, 0)
+    lax.fori_loop(0, rows // blk, stats, 0)
+
+    def scale(k, carry):
+        cols = pl.ds(pl.multiple_of(k * 128, 128), 128)
+        hat = (x_ref[:, cols].astype(F32) - mean_ref[...]) * rstd_ref[...]
+        a_ref[:, cols] = (hat * ag_ref[:, cols] + ab_ref[:, cols]).astype(BF16)
+        m_ref[:, cols] = (hat * mg_ref[:, cols] + mb_ref[:, cols]).astype(BF16)
+        return carry
+
+    lax.fori_loop(0, width // 128, scale, 0, unroll=4)
 
 
 def both_norms(x, ag, ab, mg, mb):
     rows, width = x.shape
-    blk = 64
+    blk = 128
     vec = pl.BlockSpec((1, width), lambda i: (0, 0))
     row = pl.BlockSpec((blk, width), lambda i: (i, 0))
     return pl.pallas_call(
-        functools.partial(norm_kernel, 16),
+        functools.partial(norm_kernel, 32, 256),
         grid=(rows // blk,),
         out_shape=(jax.ShapeDtypeStruct(x.shape, BF16),) * 2,
         in_specs=[row, vec, vec, vec, vec],
         out_specs=(row, row),
+        scratch_shapes=[pltpu.VMEM((blk, 128), F32)] * 2,
         compiler_params=params(),
         cost_estimate=pl.CostEstimate(flops=2 * 10 ** 10, bytes_accessed=6 * x.size, transcendentals=0),
         name="norms",
     )(x, ag, ab, mg, mb)
 
 
-def up_kernel(sub, x_ref, w_ref, o_ref):
-    def body(i, carry):
-        rows = pl.ds(pl.multiple_of(i * sub, sub), sub)
-        pre = jnp.dot(x_ref[rows, :], w_ref[...], preferred_element_type=F32)
-        o_ref[rows, :] = (0.5 * pre * (1.0 + lax.erf(pre * (2.0 ** -0.5)))).astype(BF16)
-        return carry
-
-    lax.fori_loop(0, x_ref.shape[0] // sub, body, 0)
-
-
-def up_gelu(x, w):
+def stream_rows(step, sub, copies, work):
+    parts, part = copies[0]
+
+    def cut(i, n):
+        return pl.ds(pl.multiple_of(i * n, n), n)
+
+    @pl.when(step == 0)
+    def _():
+        for i in range(parts):
+            for src, dst, sem in copies[1:]:
+                pltpu.make_async_copy(src.at[pl.ds(i * part, part), :], dst.at[pl.ds(i * part, part), :], sem.at[i]).start()
+
+        def body(i, carry):
+            for src, dst, sem in copies[1:]:
+                pltpu.make_async_copy(src.at[cut(i, part), :], dst.at[cut(i, part), :], sem.at[i]).wait()
+            work(cut(i, part))
+            return carry
+
+        lax.fori_loop(0, parts, body, 0)
+
+    @pl.when(step > 0)
+    def _():
+        def body(i, carry):
+            work(cut(i, sub))
+            return carry
+
+        lax.fori_loop(0, parts * part // sub, body, 0)
+
+
+def up_kernel(sub, parts, steps, x_hbm, y_hbm, w_ref, o_ref, x_ref, sem, y_sem):
+    step = pl.program_id(0)
+    which = step // steps
+    second = pltpu.make_async_copy(y_hbm, x_ref.at[1], y_sem)
+
+    @pl.when(step == 1)
+    def _():
+        second.start()
+
+    @pl.when(step == steps)
+    def _():
+        second.wait()
+
+    def work(rows):
+        pre = jnp.dot(x_ref[which, rows, :], w_ref[...], preferred_element_type=F32)
+        o_ref[0, rows, :] = (0.5 * pre * (1.0 + lax.erf(pre * (2.0 ** -0.5)))).astype(BF16)
+
+    stream_rows(step, sub, [(parts, x_ref.shape[1] // parts), (x_hbm, x_ref.at[0], sem)], work)
+
+
+def up_gelu(x, y, w):
     rows, depth = x.shape
     cols = w.shape[1]
     bn = 512
+    n = cols // bn
     return pl.pallas_call(
-        functools.partial(up_kernel, 384),
-        grid=(cols // bn,),
-        out_shape=jax.ShapeDtypeStruct((rows, cols), BF16),
+        functools.partial(up_kernel, 384, 4, n),
+        grid=(2 * n,),
+        out_shape=jax.ShapeDtypeStruct((2, rows, cols), BF16),
         in_specs=[
-            pl.BlockSpec((rows, depth), lambda j: (0, 0), pipeline_mode=pl.Buffered(1)),
-            pl.BlockSpec((depth, bn), lambda j: (0, j)),
+            pl.BlockSpec(memory_space=pl.ANY),
+            pl.BlockSpec(memory_space=pl.ANY),
+            pl.BlockSpec((depth, bn), lambda j: (0, j % n)),
         ],
-        out_specs=pl.BlockSpec((rows, bn), lambda j: (0, j)),
+        out_specs=pl.BlockSpec((1, rows, bn), lambda j: (j // n, 0, j % n)),
+        scratch_shapes=[pltpu.VMEM((2, rows, depth), BF16), pltpu.SemaphoreType.DMA((4,)), pltpu.SemaphoreType.DMA],
         compiler_params=params(),
-        cost_estimate=pl.CostEstimate(flops=2 * rows * depth * cols, bytes_accessed=2 * (x.size + w.size + rows * cols), transcendentals=rows * cols),
+        cost_estimate=pl.CostEstimate(flops=4 * rows * depth * cols, bytes_accessed=4 * (x.size + w.size + rows * cols), transcendentals=2 * rows * cols),
         name="up_gelu",
-    )(x, w)
+    )(x, y, w)
 
 
 def rotate(vals, cos, sin, low):
@@ -85,7 +147,7 @@
     return vals * cos + turned * sin
 
 
-def attn_kernel(blk, scale, tp_ref, r0, r1, r2, r3, cq_ref, sq_ref, ck_ref, sk_ref, o_ref, q_ref, kt_ref, v_ref):
+def attn_kernel(blk, scale, tp_ref, r0, r1, r2, r3, cq_ref, sq_ref, ck_ref, sk_ref, o_ref, q_ref, kt_ref, v_ref, pr_ref):
     t = pl.program_id(2)
     slots = (r0, r1, r2, r3)
     pairs = o_ref.shape[-1] // 128
@@ -120,19 +182,20 @@
         def _(tt=tt):
             keys = (tt + 1) * blk
 
+            def soft(s, e):
+                diag = jnp.where(allowed, s[:, keys - blk:], -1e30)
+                s = jnp.concatenate([s[:, :keys - blk], diag], axis=1) if tt else diag
+                top = jnp.max(s, axis=-1, keepdims=True)
+                ex = jnp.exp2((s - top) * (scale * LOG2E))
+                pr_ref[:, e * keys:(e + 1) * keys] = (ex * (1.0 / jnp.sum(ex, axis=-1, keepdims=True))).astype(BF16)
+
             def body(p, carry):
                 cols = pl.ds(pl.multiple_of(p * 128, 128), 128)
                 q = q_ref[:, cols]
-                ctx = None
                 for e in range(2):
-                    s = jnp.dot(q, kt_ref[e, :, :keys], preferred_element_type=F32)
-                    diag = jnp.where(allowed, s[:, keys - blk:], -1e30)
-                    s = jnp.concatenate([s[:, :keys - blk], diag], axis=1) if tt else diag
-                    top = jnp.max(s, axis=-1, keepdims=True)
-                    ex = jnp.exp2((s - top) * (scale * LOG2E))
-                    prob = (ex * (1.0 / jnp.sum(ex, axis=-1, keepdims=True))).astype(BF16)
-                    part = jnp.dot(prob, v_ref[e, :keys, :], preferred_element_type=F32)
-                    ctx = part if ctx is None else ctx + part
+                    soft(jnp.dot(q, kt_ref[e, :, :keys], preferred_element_type=F32), e)
+                vv = jnp.concatenate([v_ref[0, :keys, :], v_ref[1, :keys, :]], axis=0)
+                ctx = jnp.dot(pr_ref[:, :2 * keys], vv, preferred_element_type=F32)
                 o_ref[0, :, cols] = ctx.astype(BF16)
                 return carry
 
@@ -164,7 +227,7 @@
             grid=(batch, groups, slots),
             in_specs=[part] * slots + [tab, tab, full, full],
             out_specs=pl.BlockSpec((1, blk, qcols), lambda b, g, t, tp: (tp[0] ^ t, b, g)),
-            scratch_shapes=[pltpu.VMEM((blk, qcols), BF16), pltpu.VMEM((2, 128, tokens), BF16), pltpu.VMEM((2, tokens, 128), BF16)],
+            scratch_shapes=[pltpu.VMEM((blk, qcols), BF16), pltpu.VMEM((2, 128, tokens), BF16), pltpu.VMEM((2, tokens, 128), BF16)] + [pltpu.VMEM((blk, 2 * tokens), BF16)],
         ),
         out_shape=jax.ShapeDtypeStruct((slots, batch * blk, groups * qcols), BF16),
         compiler_params=params(),
@@ -173,23 +236,22 @@
     )(my, *qkv, cq, sq, ck, sk)
 
 
-def down_kernel(sub, n_add, h_ref, c_ref, wd_ref, wo_ref, *refs):
-    o_ref = refs[-1]
-
-    def body(i, carry):
-        rows = pl.ds(pl.multiple_of(i * sub, sub), sub)
+def down_kernel(sub, parts, slot, which, n_add, h_hbm, c_hbm, wd_ref, wo_ref, *refs):
+    o_ref, h_ref, c_ref, h_sem, c_sem = refs[-5:]
+
+    def work(rows):
         acc = jnp.dot(h_ref[rows, :], wd_ref[...], preferred_element_type=F32)
-        acc += jnp.dot(c_ref[0, rows, :], wo_ref[...], preferred_element_type=F32)
+        acc += jnp.dot(c_ref[rows, :], wo_ref[...], preferred_element_type=F32)
         for add in refs[:n_add]:
             acc += add[rows, :].astype(F32)
         o_ref[rows, :] = acc.astype(BF16)
-        return carry
-
-    lax.fori_loop(0, h_ref.shape[0] // sub, body, 0)
-
-
-def down(h, ctx, slot, wd, wo, half, adds=(), into=None, wide=False):
-    rows, depth = h.shape
+
+    copies = [(parts, h_ref.shape[0] // parts), (h_hbm.at[which], h_ref, h_sem), (c_hbm.at[slot], c_ref, c_sem)]
+    stream_rows(pl.program_id(0), sub, copies, work)
+
+
+def down(h, which, ctx, slot, wd, wo, half, adds=(), into=None, wide=False):
+    rows, depth = h.shape[1:]
     width = wd.shape[1]
     bn = 512
     n = width // 2 // bn
@@ -199,8 +261,8 @@
         return pl.BlockSpec((rows, bn), (lambda j: (0, j + off)) if is_wide else (lambda j: (0, j)))
 
     in_specs = [
-        pl.BlockSpec((rows, depth), lambda j: (0, 0), pipeline_mode=pl.Buffered(1)),
-        pl.BlockSpec((1, rows, ctx.shape[2]), lambda j: (slot, 0, 0), pipeline_mode=pl.Buffered(1)),
+        pl.BlockSpec(memory_space=pl.ANY),
+        pl.BlockSpec(memory_space=pl.ANY),
         pl.BlockSpec((depth, bn), lambda j: (0, j + off)),
         pl.BlockSpec((wo.shape[0], bn), lambda j: (0, j + off)),
     ] + [cols_spec(w) for _, w in adds]
@@ -211,11 +273,17 @@
         alias = {len(args): 0}
         args.append(into)
     return pl.pallas_call(
-        functools.partial(down_kernel, 384, len(adds)),
+        functools.partial(down_kernel, 384, 4, slot, which, len(adds)),
         grid=(n,),
         out_shape=jax.ShapeDtypeStruct((rows, width if wide else width // 2), BF16),
         in_specs=in_specs,
         out_specs=cols_spec(wide),
+        scratch_shapes=[
+            pltpu.VMEM((rows, depth), BF16),
+            pltpu.VMEM((rows, ctx.shape[2]), BF16),
+            pltpu.SemaphoreType.DMA((4,)),
+            pltpu.SemaphoreType.DMA((4,)),
+        ],
         input_output_aliases=alias,
         compiler_params=params(),
         cost_estimate=pl.CostEstimate(flops=rows * (depth + wo.shape[0]) * width, bytes_accessed=depth * width + 4 * rows * width, transcendentals=0),
@@ -242,23 +310,21 @@
         a0, m0 = both_norms(x, *vecs)
         m1 = mate(m0)
         a1 = mate(a0)
-        h0 = up_gelu(m0, w_up)
-        q0 = qkv_of(after(a0, h0))
-        h1 = up_gelu(after(m1, q0), w_up)
-        q1 = qkv_of(after(a1, h1))
+        q0 = qkv_of(a0)
+        h01 = up_gelu(m0, after(m1, q0), w_up)
+        q1 = qkv_of(after(a1, h01))
         a2, m2 = both_norms(after(x2, q1), *vecs)
         m3 = mate(m2)
         a3 = mate(a2)
-        h2 = up_gelu(m2, w_up)
-        q2 = qkv_of(after(a2, h2))
-        h3 = up_gelu(after(m3, q2), w_up)
-        q3 = qkv_of(after(a3, h3))
+        q2 = qkv_of(a2)
+        h23 = up_gelu(m2, after(m3, q2), w_up)
+        q3 = qkv_of(after(a3, h23))
 
         my = lax.axis_index('tp').astype(jnp.int32).reshape(1)
         ctx = attention([q0, q1, q2, q3], my, positions)
 
-        last, got = h3, {}
-        hs = (h0, h1, h2, h3)
+        last, got = h23, {}
+        hs = (h01, h01, h23, h23)
         out = None
         for slot in (3, 2, 1, 0):
             for s in range(2):
@@ -267,7 +333,7 @@
                     adds = ((got[3, s], False),)
                 if slot == 0:
                     adds = ((got[1, s], False), (got[2, s], False), (x, True))
-                last = down(after(hs[slot], last), ctx, slot, w_down, w_out, s, adds=adds, into=out, wide=slot == 0)
+                last = down(after(hs[slot], last), slot % 2, ctx, slot, w_down, w_out, s, adds=adds, into=out, wide=slot == 0)
                 if slot == 0:
                     out = last
                 else:

time: 1630 us -> 1610 us (0.988)
  Pallas kernels: 1340 us -> 1310 us
    pallas_call x14 -> x12, Pallas kernels: 1160 us -> 1140 us  [the longest x8 626 us: down(): pl.pallas_call(functools.partial(down_kernel, 384, 4, slot, which, len(ad...]
  transfers between devices with their start and end apart: 11 -> 11, of which waited for: 2 -> 2; matrix products, arithmetic and copies ran while one was open for 8% -> 8% of each run, Pallas kernels for 50% -> 48%
where the time goes in v2:
time: 1610 us; the launch traced here: 1600 us
  Pallas kernels  1310 us (81%)
  matrix products  159 us (10%)
  waiting for transfers between devices  113 us (7%)
    pallas_call x8, Pallas kernels, down(): pl.pallas_call(functools.partial(down_kernel, 384, 4, slot, which, len(ad...  626 us
    pallas_call x2, Pallas kernels, up_gelu(): pl.pallas_call(functools.partial(up_kernel, 384, 4, n), grid=(2 * n,), ou...  461 us
    pallas_call x1, Pallas kernels, attention(): pl.pallas_call(functools.partial(attn_kernel, blk, head ** (-0.5)), grid_...  175 us
    dot_general x4, matrix products, qkv_of(): jnp.einsum('bsd,dkc->bksc', a.reshape(batch, blk, width), w_qkv, preferre...  159 us
    ppermute x6, waiting for transfers between devices, local_layer(): got[slot, s] = (over if slot == 2 else mate)(last)  113 us
    pallas_call x2, Pallas kernels, both_norms(): pl.pallas_call(functools.partial(norm_kernel, 32, 256), grid=(rows // blk...  52.4 us
  transfers between devices with their start and end apart: 11, of which 2 were waited for; matrix products, arithmetic and copies ran while one was open for 8% of the time, Pallas kernels for 48%

profile of v2, /device:TPU:0, one launch (start us, length us, event | category | flops | bytes accessed | tf_op | source)
XLA Modules:
  0.0 1597.9 jit_solution(16284892089245732274)
XLA Ops:
  0.0 26.2 %norms.2 = (bf16[768,8192]{1,0:T(8,128)(2,1)}, bf16[768,8192]{1,0:T(8,128)(2,1)}) custom-call(bf16[768,8192]{1,0:T(8,128)(2,1)} %bitcast.67, f32[1,8192]{1,0:T(1,128)} %bitcast.73, f32[1,8192]{1,0:T(1,128)} %bitcast.75, f32[1,8192]{1,0:T(1,128)} %bitcast.77, f32[1,8192]{1,0:T(1,128)} %bitcast.79), custom_call_target="tpu_custom_call" | custom-call | flops 20000000000 | bytes 37748736 | tf_op jit(solution)/shard_map/norms/pallas_call | solution.py:61
  26.2 0.8 collective-permute-start
  27.0 2.5 collective-permute-start.1
  29.7 39.5 %fusion.33.r0 = bf16[3,2,256,1152]{3,2,1,0:T(8,128)(2,1)} fusion(bf16[3,256,8192,1]{2,1,3,0:T(8,128)(2,1)} %bitcast.72, bf16[8192,2,1152]{2,1,0:T(2,128)(2,1)} %param.15), kind=kOutput, calls=%fused_computation.19 | convolution fusion | flops 28992798720 | bytes 53870592 | tf_op jit(solution)/shard_map/bsd,dkc->bksc/dot_general | solution.py:304
  69.2 230.7 %up_gelu.2.h_hbm = bf16[2,768,8192]{2,1,0:T(8,128)(2,1)} custom-call(bf16[768,8192]{1,0:T(8,128)(2,1)} %get-tuple-element.22.x_hbm, bf16[768,8192]{1,0:T(8,128)(2,1)} %collective-permute-done.y_hbm, bf16[8192,8192]{1,0:T(8,128)(2,1)} %w_ref.3), custom_call_target="tpu_custom_call" | custom-call | flops 206158430208 | bytes 318767104 | tf_op jit(solution)/shard_map/up_gelu/pallas_call | solution.py:128
  299.9 39.6 %fusion.30.r1 = bf16[3,2,256,1152]{3,2,1,0:T(8,128)(2,1)} fusion(bf16[3,256,8192,1]{2,1,3,0:T(8,128)(2,1)} %bitcast.12, bf16[8192,2,1152]{2,1,0:T(2,128)(2,1)} %param.15), kind=kOutput, calls=%fused_computation.18 | convolution fusion | flops 28992798720 | bytes 53870592 | tf_op jit(solution)/shard_map/bsd,dkc->bksc/dot_general | solution.py:304
  339.5 26.2 %norms.3 = (bf16[768,8192]{1,0:T(8,128)(2,1)}, bf16[768,8192]{1,0:T(8,128)(2,1)}) custom-call(bf16[768,8192]{1,0:T(8,128)(2,1)} %collective-permute-done.1.x_ref, f32[1,8192]{1,0:T(1,128)} %bitcast.74, f32[1,8192]{1,0:T(1,128)} %bitcast.76, f32[1,8192]{1,0:T(1,128)} %bitcast.78, f32[1,8192]{1,0:T(1,128)} %bitcast.80), custom_call_target="tpu_custom_call" | custom-call | flops 20000000000 | bytes 37748736 | tf_op jit(solution)/shard_map/norms/pallas_call | solution.py:61
  366.2 1.9 fusion.38
  368.1 2.1 fusion.36
  370.5 39.7 %fusion.27.r2 = bf16[3,2,256,1152]{3,2,1,0:T(8,128)(2,1)} fusion(bf16[3,256,8192,1]{2,1,3,0:T(8,128)(2,1)} %bitcast.71, bf16[8192,2,1152]{2,1,0:T(2,128)(2,1)} %param.15), kind=kOutput, calls=%fused_computation.17 | convolution fusion | flops 28992798720 | bytes 53870592 | tf_op jit(solution)/shard_map/bsd,dkc->bksc/dot_general | solution.py:304
  410.2 230.6 %up_gelu.3.h_hbm = bf16[2,768,8192]{2,1,0:T(8,128)(2,1)} custom-call(bf16[768,8192]{1,0:T(8,128)(2,1)} %get-tuple-element.27.x_hbm, bf16[768,8192]{1,0:T(8,128)(2,1)} %collective-permute-done.3.y_hbm, bf16[8192,8192]{1,0:T(8,128)(2,1)} %w_ref.3), custom_call_target="tpu_custom_call" | custom-call | flops 206158430208 | bytes 318767104 | tf_op jit(solution)/shard_map/up_gelu/pallas_call | solution.py:128
  640.9 39.8 %fusion.24.r3 = bf16[3,2,256,1152]{3,2,1,0:T(8,128)(2,1)} fusion(bf16[3,256,8192,1]{2,1,3,0:T(8,128)(2,1)} %bitcast.23, bf16[8192,2,1152]{2,1,0:T(2,128)(2,1)} %param.15), kind=kOutput, calls=%fused_computation.16 | convolution fusion | flops 28992798720 | bytes 53870592 | tf_op jit(solution)/shard_map/bsd,dkc->bksc/dot_general | solution.py:304
  680.7 175.1 %attention.1.c_hbm = bf16[4,768,2048]{2,1,0:T(8,128)(2,1)} custom-call(s32[1]{0:T(128)} %bitcast.20.tp_ref, bf16[3,2,256,1152]{3,2,1,0:T(8,128)(2,1)} %fusion.33.r0, bf16[3,2,256,1152]{3,2,1,0:T(8,128)(2,1)} %fusion.30.r1, bf16[3,2,256,1152]{3,2,1,0:T(8,128)(2,1)} %fusion.27.r2, bf16[3,2,256,1152]{3,2,1,0:T(8,128)(2,1)} %fusion.24.r3, ...), custom_call_target="tpu_custom_call" | custom-call | flops 50331648000 | bytes 14155776 | tf_op jit(solution)/shard_map/attention/pallas_call | solution.py:223
  855.7 77.2 %down.8 = bf16[768,4096]{1,0:T(8,128)(2,1)} custom-call(bf16[2,768,8192]{2,1,0:T(8,128)(2,1)} %up_gelu.3.h_hbm, bf16[4,768,2048]{2,1,0:T(8,128)(2,1)} %attention.1.c_hbm, bf16[8192,8192]{1,0:T(8,128)(2,1)} %wd_ref.15, bf16[2048,8192]{1,0:T(8,128)(2,1)} %wo_ref.15), custom_call_target="tpu_custom_call" | custom-call | flops 64424509440 | bytes 92274688 | tf_op jit(solution)/shard_map/down/pallas_call | solution.py:275
  933.2 77.4 %down.9 = bf16[768,4096]{1,0:T(8,128)(2,1)} custom-call(bf16[2,768,8192]{2,1,0:T(8,128)(2,1)} %up_gelu.3.h_hbm, bf16[4,768,2048]{2,1,0:T(8,128)(2,1)} %attention.1.c_hbm, bf16[8192,8192]{1,0:T(8,128)(2,1)} %wd_ref.15, bf16[2048,8192]{1,0:T(8,128)(2,1)} %wo_ref.15), custom_call_target="tpu_custom_call" | custom-call | flops 64424509440 | bytes 92274688 | tf_op jit(solution)/shard_map/down/pallas_call | solution.py:275
  1010.9 77.8 %down.10 = bf16[768,4096]{1,0:T(8,128)(2,1)} custom-call(bf16[2,768,8192]{2,1,0:T(8,128)(2,1)} %up_gelu.3.h_hbm, bf16[4,768,2048]{2,1,0:T(8,128)(2,1)} %attention.1.c_hbm, bf16[8192,8192]{1,0:T(8,128)(2,1)} %wd_ref.15, bf16[2048,8192]{1,0:T(8,128)(2,1)} %wo_ref.15, bf16[768,4096]{1,0:T(8,128)(2,1)} %collective-permute-done.5.refs_0_), custom_call_target="tpu_custom_call" | custom-call | flops 64424509440 | bytes 92274688 | tf_op jit(solution)/shard_map/down/pallas_call | solution.py:275
  1088.7 77.8 %down.11 = bf16[768,4096]{1,0:T(8,128)(2,1)} custom-call(bf16[2,768,8192]{2,1,0:T(8,128)(2,1)} %up_gelu.3.h_hbm, bf16[4,768,2048]{2,1,0:T(8,128)(2,1)} %attention.1.c_hbm, bf16[8192,8192]{1,0:T(8,128)(2,1)} %wd_ref.15, bf16[2048,8192]{1,0:T(8,128)(2,1)} %wo_ref.15, bf16[768,4096]{1,0:T(8,128)(2,1)} %collective-permute-done.6.refs_0_), custom_call_target="tpu_custom_call" | custom-call | flops 64424509440 | bytes 92274688 | tf_op jit(solution)/shard_map/down/pallas_call | solution.py:275
  1166.5 77.4 %down.12 = bf16[768,4096]{1,0:T(8,128)(2,1)} custom-call(bf16[2,768,8192]{2,1,0:T(8,128)(2,1)} %up_gelu.2.h_hbm, bf16[4,768,2048]{2,1,0:T(8,128)(2,1)} %attention.1.c_hbm, bf16[8192,8192]{1,0:T(8,128)(2,1)} %wd_ref.15, bf16[2048,8192]{1,0:T(8,128)(2,1)} %wo_ref.15), custom_call_target="tpu_custom_call" | custom-call | flops 64424509440 | bytes 92274688 | tf_op jit(solution)/shard_map/down/pallas_call | solution.py:275
  1244.3 77.3 %down.13 = bf16[768,4096]{1,0:T(8,128)(2,1)} custom-call(bf16[2,768,8192]{2,1,0:T(8,128)(2,1)} %up_gelu.2.h_hbm, bf16[4,768,2048]{2,1,0:T(8,128)(2,1)} %attention.1.c_hbm, bf16[8192,8192]{1,0:T(8,128)(2,1)} %wd_ref.15, bf16[2048,8192]{1,0:T(8,128)(2,1)} %wo_ref.15), custom_call_target="tpu_custom_call" | custom-call | flops 64424509440 | bytes 92274688 | tf_op jit(solution)/shard_map/down/pallas_call | solution.py:275
  1321.9 1.8 collective-permute-start.10
  1323.7 59.3 %collective-permute-done.8.refs_1_ = bf16[768,4096]{1,0:T(8,128)(2,1)} collective-permute-done((bf16[768,4096]{1,0:T(8,128)(2,1)}, bf16[768,4096]{1,0:T(8,128)(2,1)}, u32[]{:S(2)}, u32[]{:S(2)}) %collective-permute-start.8) | collective-permute-done | bytes 6291488 | tf_op jit(solution)/shard_map/ppermute | solution.py:340
  1382.9 80.7 %down.14.refs_3_ = bf16[768,8192]{1,0:T(8,128)(2,1)} custom-call(bf16[2,768,8192]{2,1,0:T(8,128)(2,1)} %up_gelu.2.h_hbm, bf16[4,768,2048]{2,1,0:T(8,128)(2,1)} %attention.1.c_hbm, bf16[8192,8192]{1,0:T(8,128)(2,1)} %wd_ref.15, bf16[2048,8192]{1,0:T(8,128)(2,1)} %wo_ref.15, bf16[768,4096]{1,0:T(8,128)(2,1)} %collective-permute-done.7.refs_0_, ...), custom_call_target="tpu_custom_call" | custom-call | flops 64424509440 | bytes 92274688 | tf_op jit(solution)/shard_map/down/pallas_call | solution.py:275
  1463.7 53.4 %collective-permute-done.10.refs_1_ = bf16[768,4096]{1,0:T(8,128)(2,1)} collective-permute-done((bf16[768,4096]{1,0:T(8,128)(2,1)}, bf16[768,4096]{1,0:T(8,128)(2,1)}, u32[]{:S(2)}, u32[]{:S(2)}) %collective-permute-start.10) | collective-permute-done | bytes 6291488 | tf_op jit(solution)/shard_map/ppermute | solution.py:340
  1517.1 80.3 %down.15 = bf16[768,8192]{1,0:T(8,128)(2,1)} custom-call(bf16[2,768,8192]{2,1,0:T(8,128)(2,1)} %up_gelu.2.h_hbm, bf16[4,768,2048]{2,1,0:T(8,128)(2,1)} %attention.1.c_hbm, bf16[8192,8192]{1,0:T(8,128)(2,1)} %wd_ref.15, bf16[2048,8192]{1,0:T(8,128)(2,1)} %wo_ref.15, bf16[768,4096]{1,0:T(8,128)(2,1)} %collective-permute-done.9.refs_0_, ...), custom_call_target="tpu_custom_call", output_to_operand_aliasing={{}: (7, {})} | custom-call | flops 64424509440 | bytes 92274688 | tf_op jit(solution)/shard_map/down/pallas_call | solution.py:275
  (25 shorter events, 2.0 us)
Async XLA Ops:
  26.2 43.1 %collective-permute-start = (bf16[768,8192]{1,0:T(8,128)(2,1)}, bf16[768,8192]{1,0:T(8,128)(2,1)}, u32[]{:S(2)}, u32[]{:S(2)}) collective-permute-start(bf16[768,8192]{1,0:T(8,128)(2,1)} %get-tuple-element.22.x_hbm), channel_id=1, source_target_pairs={{0,1},{1,0},{2,3},{3,2},{4,5},{5,4},{6,7},{7,6}} | collective-permute-start | bytes 37748744 | tf_op jit(solution)/shard_map/ppermute | solution.py:311
  27.0 312.5 %collective-permute-start.1 = (bf16[768,8192]{1,0:T(8,128)(2,1)}, bf16[768,8192]{1,0:T(8,128)(2,1)}, u32[]{:S(2)}, u32[]{:S(2)}) collective-permute-start(bf16[768,8192]{1,0:T(8,128)(2,1)} %bitcast.68), channel_id=1, source_target_pairs={{0,2},{1,3},{2,0},{3,1},{4,6},{5,7},{6,4},{7,5}} | collective-permute-start | bytes 37748744 | tf_op jit(solution)/shard_map/ppermute | solution.py:309
  29.5 270.4 %collective-permute-start.2 = (bf16[768,8192]{1,0:T(8,128)(2,1)}, bf16[768,8192]{1,0:T(8,128)(2,1)}, u32[]{:S(2)}, u32[]{:S(2)}) collective-permute-start(bf16[768,8192]{1,0:T(8,128)(2,1)} %get-tuple-element.23), channel_id=1, source_target_pairs={{0,1},{1,0},{2,3},{3,2},{4,5},{5,4},{6,7},{7,6}} | collective-permute-start | bytes 37748744 | tf_op jit(solution)/shard_map/ppermute | solution.py:312
  339.5 26.5 %copy-start = (s32[1024]{0:T(1024)S(1)}, s32[1024]{0:T(1024)}, u32[]{:S(2)}) copy-start(s32[1024]{0:T(1024)} %param.19) | copy-start | bytes 12292
  365.7 44.5 %collective-permute-start.3 = (bf16[768,8192]{1,0:T(8,128)(2,1)}, bf16[768,8192]{1,0:T(8,128)(2,1)}, u32[]{:S(2)}, u32[]{:S(2)}) collective-permute-start(bf16[768,8192]{1,0:T(8,128)(2,1)} %get-tuple-element.27.x_hbm), channel_id=1, source_target_pairs={{0,1},{1,0},{2,3},{3,2},{4,5},{5,4},{6,7},{7,6}} | collective-permute-start | bytes 37748744 | tf_op jit(solution)/shard_map/ppermute | solution.py:317
  370.2 270.6 %collective-permute-start.4 = (bf16[768,8192]{1,0:T(8,128)(2,1)}, bf16[768,8192]{1,0:T(8,128)(2,1)}, u32[]{:S(2)}, u32[]{:S(2)}) collective-permute-start(bf16[768,8192]{1,0:T(8,128)(2,1)} %get-tuple-element.28), channel_id=1, source_target_pairs={{0,1},{1,0},{2,3},{3,2},{4,5},{5,4},{6,7},{7,6}} | collective-permute-start | bytes 37748744 | tf_op jit(solution)/shard_map/ppermute | solution.py:318
  933.0 78.0 %collective-permute-start.5 = (bf16[768,4096]{1,0:T(8,128)(2,1)}, bf16[768,4096]{1,0:T(8,128)(2,1)}, u32[]{:S(2)}, u32[]{:S(2)}) collective-permute-start(bf16[768,4096]{1,0:T(8,128)(2,1)} %down.8), channel_id=1, source_target_pairs={{0,1},{1,0},{2,3},{3,2},{4,5},{5,4},{6,7},{7,6}} | collective-permute-start | bytes 18874376 | tf_op jit(solution)/shard_map/ppermute | solution.py:340
  1010.7 78.1 %collective-permute-start.6 = (bf16[768,4096]{1,0:T(8,128)(2,1)}, bf16[768,4096]{1,0:T(8,128)(2,1)}, u32[]{:S(2)}, u32[]{:S(2)}) collective-permute-start(bf16[768,4096]{1,0:T(8,128)(2,1)} %down.9), channel_id=1, source_target_pairs={{0,1},{1,0},{2,3},{3,2},{4,5},{5,4},{6,7},{7,6}} | collective-permute-start | bytes 18874376 | tf_op jit(solution)/shard_map/ppermute | solution.py:340
  1244.0 79.7 %collective-permute-start.7 = (bf16[768,4096]{1,0:T(8,128)(2,1)}, bf16[768,4096]{1,0:T(8,128)(2,1)}, u32[]{:S(2)}, u32[]{:S(2)}) collective-permute-start(bf16[768,4096]{1,0:T(8,128)(2,1)} %down.12), channel_id=1, source_target_pairs={{0,1},{1,0},{2,3},{3,2},{4,5},{5,4},{6,7},{7,6}} | collective-permute-start | bytes 18874376 | tf_op jit(solution)/shard_map/ppermute | solution.py:340
  1244.2 138.7 %collective-permute-start.8 = (bf16[768,4096]{1,0:T(8,128)(2,1)}, bf16[768,4096]{1,0:T(8,128)(2,1)}, u32[]{:S(2)}, u32[]{:S(2)}) collective-permute-start(bf16[768,4096]{1,0:T(8,128)(2,1)} %down.10), channel_id=1, source_target_pairs={{0,2},{1,3},{2,0},{3,1},{4,6},{5,7},{6,4},{7,5}} | collective-permute-start | bytes 18874376 | tf_op jit(solution)/shard_map/ppermute | solution.py:340
  1321.7 142.0 %collective-permute-start.9 = (bf16[768,4096]{1,0:T(8,128)(2,1)}, bf16[768,4096]{1,0:T(8,128)(2,1)}, u32[]{:S(2)}, u32[]{:S(2)}) collective-permute-start(bf16[768,4096]{1,0:T(8,128)(2,1)} %down.13), channel_id=1, source_target_pairs={{0,1},{1,0},{2,3},{3,2},{4,5},{5,4},{6,7},{7,6}} | collective-permute-start | bytes 18874376 | tf_op jit(solution)/shard_map/ppermute | solution.py:340
  1321.9 195.2 %collective-permute-start.10 = (bf16[768,4096]{1,0:T(8,128)(2,1)}, bf16[768,4096]{1,0:T(8,128)(2,1)}, u32[]{:S(2)}, u32[]{:S(2)}) collective-permute-start(bf16[768,4096]{1,0:T(8,128)(2,1)} %down.11), channel_id=1, source_target_pairs={{0,2},{1,3},{2,0},{3,1},{4,6},{5,7},{6,4},{7,5}} | collective-permute-start | bytes 18874376 | tf_op jit(solution)/shard_map/ppermute | solution.py:340
